TPU v7x, 32 devices: a whole 2x2x4 slice. The times are simulated.
32 devices in a mesh: gx: 4 (over x, core), gy: 4 (over z), gz: 2 (over y).
Axes of the slice: x: 2, y: 2, z: 4, core: 2. Of those that a mesh axis runs over, the one named last changes fastest.
Arguments:
- density: float32 [32, 64, 256], P('gx', 'gy', 'gz'), may hold values from 0.1 to 10
- x_faces: float32 [2, 64, 256], P(None, 'gy', 'gz'), may hold values from -6 to 6
- y_faces: float32 [2, 32, 256], P(None, 'gx', 'gz'), may hold values from -6 to 6
- z_faces: float32 [2, 32, 64], P(None, 'gx', 'gy'), may hold values from -6 to 6
Outputs:
- solution_field: float32 [32, 64, 256], P('gx', 'gy', 'gz')
- residual: float32 [32, 64, 256], P('gx', 'gy', 'gz')
All inputs are finite; a program needn't handle non-finite values.
Results may differ from a plain program's by a relative error of at most 0.0003.
Values sent between devices are 32-bit elements; how exact they have to be, the bound alone decides.
A program may use at most 64 MiB of HBM per device.

v0:
```python
import jax
import jax.numpy as jnp
from jax import lax
from jax.sharding import PartitionSpec as P

ITERS = 2
LEVELS = 3
COARSE_SWEEPS = 3


relax_rate = 1.0 / 9.0
coupling = 0.5


def padded_2(cells, sides, width):
    for axis, dim in sides:
        count = lax.axis_size(axis)
        ends = count - 1
        head = lax.slice_in_dim(cells, 0, width, axis=dim)
        tail = lax.slice_in_dim(cells, cells.shape[dim] - width, cells.shape[dim], axis=dim)
        cells = jnp.concatenate(
            [
                lax.ppermute(tail, axis, [(i, (i + 1) % count) for i in range(ends)]),
                cells,
                lax.ppermute(head, axis, [((i + 1) % count, i) for i in range(ends)]),
            ],
            axis=dim,
        )
    return cells


def beside_sum(padded):
    beside = padded[2:, 1:-1, 1:-1] + padded[:-2, 1:-1, 1:-1]
    beside = beside + padded[1:-1, 2:, 1:-1] + padded[1:-1, :-2, 1:-1]
    beside = beside + padded[1:-1, 1:-1, 2:] + padded[1:-1, 1:-1, :-2]
    return beside


def operate(field):
    padded = padded_2(field, (("gx", 0), ("gy", 1), ("gz", 2)), 1)
    return 6.0 * field - beside_sum(padded)


def restrict(field):
    sx, sy, sz = field.shape
    return 0.5 * jnp.sum(field.reshape(sx // 2, 2, sy // 2, 2, sz // 2, 2), axis=(1, 3, 5))


def prolong(field):
    sx, sy, sz = field.shape
    spread = jnp.broadcast_to(field[:, None, :, None, :, None], (sx, 2, sy, 2, sz, 2))
    return spread.reshape(2 * sx, 2 * sy, 2 * sz)


def coarse_solve(right_side):
    approx = relax_rate * right_side
    for sweep_idx in range(COARSE_SWEEPS - 1):
        approx = approx + relax_rate * (right_side - operate(approx))
    return approx


def cycle(right_side, level_idx):
    if level_idx == LEVELS - 1:
        return coarse_solve(right_side)
    approx = relax_rate * right_side
    defect = right_side - operate(approx)
    approx = approx + prolong(cycle(restrict(defect), level_idx + 1))
    return approx + relax_rate * (right_side - operate(approx))


def precondition_image(residual):
    approx = relax_rate * residual
    defect = residual - operate(approx)
    approx = approx + prolong(cycle(restrict(defect), 1))
    precond = approx + relax_rate * (residual - operate(approx))
    return (precond, operate(precond))


def joint_sums(residual, precond, precond_image):
    return lax.psum(
        (jnp.sum(residual * precond), jnp.sum(precond * precond_image)), ("gx", "gy", "gz")
    )


def local(density, x_faces, y_faces, z_faces):
    right_side = -coupling * density
    right_side = right_side.at[0].add(jnp.where(lax.axis_index("gx") == 0, x_faces[0], 0.0))
    right_side = right_side.at[-1].add(
        jnp.where(lax.axis_index("gx") == lax.axis_size("gx") - 1, x_faces[1], 0.0)
    )
    right_side = right_side.at[:, 0].add(jnp.where(lax.axis_index("gy") == 0, y_faces[0], 0.0))
    right_side = right_side.at[:, -1].add(
        jnp.where(lax.axis_index("gy") == lax.axis_size("gy") - 1, y_faces[1], 0.0)
    )
    right_side = right_side.at[:, :, 0].add(jnp.where(lax.axis_index("gz") == 0, z_faces[0], 0.0))
    right_side = right_side.at[:, :, -1].add(
        jnp.where(lax.axis_index("gz") == lax.axis_size("gz") - 1, z_faces[1], 0.0)
    )
    solution_field = jnp.zeros_like(right_side)
    residual = right_side
    precond, pimage = precondition_image(residual)
    gamma_now, delta_now = joint_sums(residual, precond, pimage)
    step_size = gamma_now / delta_now
    direction = precond
    image = pimage
    for iteration in range(ITERS):
        solution_field = solution_field + step_size * direction
        residual = residual - step_size * image
        if iteration + 1 < ITERS:
            precond, pimage = precondition_image(residual)
            gamma_next, delta_now = joint_sums(residual, precond, pimage)
            growth = gamma_next / gamma_now
            step_size = gamma_next / (delta_now - growth * gamma_next / step_size)
            direction = precond + growth * direction
            image = pimage + growth * image
            gamma_now = gamma_next
    return (solution_field, residual)


def solution(mesh):
    placed = (P("gx", "gy", "gz"), P(None, "gy", "gz"), P(None, "gx", "gz"), P(None, "gx", "gy"))
    return jax.shard_map(
        local,
        mesh=mesh,
        in_specs=placed,
        out_specs=(P("gx", "gy", "gz"), P("gx", "gy", "gz")),
        check_vma=False,
    )
```

profile of v0, /device:TPU:0, one launch (start us, length us, event | category | flops | bytes accessed | tf_op | source)
XLA Modules:
  0.0 447.0 jit_solution(14585865203178151071)
XLA Ops:
  18.0 4.2 collective-permute-done.2
  23.6 4.6 %collective-permute-start.5 = (f32[10,18,1]{2,1,0:T(8,128)S(1)}, f32[10,18,1]{2,1,0:T(8,128)S(1)}, u32[]{:S(2)}, u32[]{:S(2)}) collective-permute-start(f32[10,18,1]{2,1,0:T(8,128)S(1)} %get-tuple-element.101), channel_id=1, source_target_pairs={{0,1},{2,3},{4,5},{6,7},{8,9},{10,11},{12,13},{14,15},{16,17},{18,... | collective-permute-start | bytes 2168 | tf_op jit(solution)/shard_map/ppermute | solution.py:23
  31.7 5.5 %reshape.240 = f32[4,2,8,2,64,2]{5,4,3,2,1,0:T(8,128)} reshape(f32[8,16,128]{2,1,0:T(8,128)S(1)} %fusion.39) | data formatting | bytes 131072 | tf_op jit(solution)/shard_map/reshape | solution.py:46
  56.1 4.5 %collective-permute-start.11 = (f32[6,10,1]{2,1,0:T(8,128)S(1)}, f32[6,10,1]{2,1,0:T(8,128)S(1)}, u32[]{:S(2)}, u32[]{:S(2)}) collective-permute-start(f32[6,10,1]{2,1,0:T(8,128)S(1)} %get-tuple-element.133), channel_id=1, source_target_pairs={{0,1},{2,3},{4,5},{6,7},{8,9},{10,11},{12,13},{14,15},{16,17},{18,... | collective-permute-start | bytes 728 | tf_op jit(solution)/shard_map/ppermute | solution.py:23
  80.4 4.5 %collective-permute-start.17 = (f32[4,6,1]{2,1,0:T(8,128)S(1)}, f32[4,6,1]{2,1,0:T(8,128)S(1)}, u32[]{:S(2)}, u32[]{:S(2)}) collective-permute-start(f32[4,6,1]{2,1,0:T(8,128)S(1)} %get-tuple-element.155), channel_id=1, source_target_pairs={{0,1},{2,3},{4,5},{6,7},{8,9},{10,11},{12,13},{14,15},{16,17},{18,... | collective-permute-start | bytes 296 | tf_op jit(solution)/shard_map/ppermute | solution.py:23
  102.2 4.5 %collective-permute-start.23 = (f32[4,6,1]{2,1,0:T(8,128)S(1)}, f32[4,6,1]{2,1,0:T(8,128)S(1)}, u32[]{:S(2)}, u32[]{:S(2)}) collective-permute-start(f32[4,6,1]{2,1,0:T(8,128)S(1)} %get-tuple-element.153), channel_id=1, source_target_pairs={{0,1},{2,3},{4,5},{6,7},{8,9},{10,11},{12,13},{14,15},{16,17},{18,... | collective-permute-start | bytes 296 | tf_op jit(solution)/shard_map/ppermute | solution.py:23
  124.3 4.5 %collective-permute-start.29 = (f32[6,10,1]{2,1,0:T(8,128)S(1)}, f32[6,10,1]{2,1,0:T(8,128)S(1)}, u32[]{:S(2)}, u32[]{:S(2)}) collective-permute-start(f32[6,10,1]{2,1,0:T(8,128)S(1)} %get-tuple-element.131), channel_id=1, source_target_pairs={{0,1},{2,3},{4,5},{6,7},{8,9},{10,11},{12,13},{14,15},{16,17},{18,... | collective-permute-start | bytes 728 | tf_op jit(solution)/shard_map/ppermute | solution.py:23
  147.5 4.2 collective-permute-done.32
  153.1 4.6 %collective-permute-start.35 = (f32[10,18,1]{2,1,0:T(8,128)S(1)}, f32[10,18,1]{2,1,0:T(8,128)S(1)}, u32[]{:S(2)}, u32[]{:S(2)}) collective-permute-start(f32[10,18,1]{2,1,0:T(8,128)S(1)} %get-tuple-element.99), channel_id=1, source_target_pairs={{0,1},{2,3},{4,5},{6,7},{8,9},{10,11},{12,13},{14,15},{16,17},{18,... | collective-permute-start | bytes 2168 | tf_op jit(solution)/shard_map/ppermute | solution.py:23
  170.4 4.2 collective-permute-done.38
  176.1 4.6 %collective-permute-start.41 = (f32[10,18,1]{2,1,0:T(8,128)S(1)}, f32[10,18,1]{2,1,0:T(8,128)S(1)}, u32[]{:S(2)}, u32[]{:S(2)}) collective-permute-start(f32[10,18,1]{2,1,0:T(8,128)S(1)} %get-tuple-element.97), channel_id=1, source_target_pairs={{0,1},{2,3},{4,5},{6,7},{8,9},{10,11},{12,13},{14,15},{16,17},{18,... | collective-permute-start | bytes 2168 | tf_op jit(solution)/shard_map/ppermute | solution.py:23
  184.9 39.6 %all-reduce.1 = (f32[]{:T(128)}, f32[]{:T(128)}) all-reduce(f32[]{:T(128)} %get-tuple-element.81, f32[]{:T(128)} %get-tuple-element.80), channel_id=1, replica_groups=mesh['gx'=4,'gy'=4,'gz'=2] {'gx','gy','gz'}, use_global_device_ids=true, to_apply=%region_3.4 | all-reduce | flops 2 | bytes 16 | tf_op jit(solution)/shard_map/psum | solution.py:80
  228.4 4.3 collective-permute-done.42
  237.9 4.2 collective-permute-done.44
  243.6 4.6 %collective-permute-start.47 = (f32[10,18,1]{2,1,0:T(8,128)S(1)}, f32[10,18,1]{2,1,0:T(8,128)S(1)}, u32[]{:S(2)}, u32[]{:S(2)}) collective-permute-start(f32[10,18,1]{2,1,0:T(8,128)S(1)} %get-tuple-element.95), channel_id=1, source_target_pairs={{0,1},{2,3},{4,5},{6,7},{8,9},{10,11},{12,13},{14,15},{16,17},{18,... | collective-permute-start | bytes 2168 | tf_op jit(solution)/shard_map/ppermute | solution.py:23
  251.7 5.5 %reshape.244 = f32[4,2,8,2,64,2]{5,4,3,2,1,0:T(8,128)} reshape(f32[8,16,128]{2,1,0:T(8,128)S(1)} %fusion.17) | data formatting | bytes 131072 | tf_op jit(solution)/shard_map/reshape | solution.py:46
  275.2 4.7 %collective-permute-start.53 = (f32[6,10,1]{2,1,0:T(8,128)S(1)}, f32[6,10,1]{2,1,0:T(8,128)S(1)}, u32[]{:S(2)}, u32[]{:S(2)}) collective-permute-start(f32[6,10,1]{2,1,0:T(8,128)S(1)} %get-tuple-element.129), channel_id=1, source_target_pairs={{0,1},{2,3},{4,5},{6,7},{8,9},{10,11},{12,13},{14,15},{16,17},{18,... | collective-permute-start | bytes 728 | tf_op jit(solution)/shard_map/ppermute | solution.py:23
  297.9 4.5 %collective-permute-start.59 = (f32[4,6,1]{2,1,0:T(8,128)S(1)}, f32[4,6,1]{2,1,0:T(8,128)S(1)}, u32[]{:S(2)}, u32[]{:S(2)}) collective-permute-start(f32[4,6,1]{2,1,0:T(8,128)S(1)} %get-tuple-element.147), channel_id=1, source_target_pairs={{0,1},{2,3},{4,5},{6,7},{8,9},{10,11},{12,13},{14,15},{16,17},{18,... | collective-permute-start | bytes 296 | tf_op jit(solution)/shard_map/ppermute | solution.py:23
  319.6 4.5 %collective-permute-start.65 = (f32[4,6,1]{2,1,0:T(8,128)S(1)}, f32[4,6,1]{2,1,0:T(8,128)S(1)}, u32[]{:S(2)}, u32[]{:S(2)}) collective-permute-start(f32[4,6,1]{2,1,0:T(8,128)S(1)} %get-tuple-element.145), channel_id=1, source_target_pairs={{0,1},{2,3},{4,5},{6,7},{8,9},{10,11},{12,13},{14,15},{16,17},{18,... | collective-permute-start | bytes 296 | tf_op jit(solution)/shard_map/ppermute | solution.py:23
  341.8 4.5 %collective-permute-start.71 = (f32[6,10,1]{2,1,0:T(8,128)S(1)}, f32[6,10,1]{2,1,0:T(8,128)S(1)}, u32[]{:S(2)}, u32[]{:S(2)}) collective-permute-start(f32[6,10,1]{2,1,0:T(8,128)S(1)} %get-tuple-element.127), channel_id=1, source_target_pairs={{0,1},{2,3},{4,5},{6,7},{8,9},{10,11},{12,13},{14,15},{16,17},{18,... | collective-permute-start | bytes 728 | tf_op jit(solution)/shard_map/ppermute | solution.py:23
  365.0 4.2 collective-permute-done.74
  370.6 4.6 %collective-permute-start.77 = (f32[10,18,1]{2,1,0:T(8,128)S(1)}, f32[10,18,1]{2,1,0:T(8,128)S(1)}, u32[]{:S(2)}, u32[]{:S(2)}) collective-permute-start(f32[10,18,1]{2,1,0:T(8,128)S(1)} %get-tuple-element.93), channel_id=1, source_target_pairs={{0,1},{2,3},{4,5},{6,7},{8,9},{10,11},{12,13},{14,15},{16,17},{18,... | collective-permute-start | bytes 2168 | tf_op jit(solution)/shard_map/ppermute | solution.py:23
  393.5 4.6 %collective-permute-start.83 = (f32[10,18,1]{2,1,0:T(8,128)S(1)}, f32[10,18,1]{2,1,0:T(8,128)S(1)}, u32[]{:S(2)}, u32[]{:S(2)}) collective-permute-start(f32[10,18,1]{2,1,0:T(8,128)S(1)} %get-tuple-element.91), channel_id=1, source_target_pairs={{0,1},{2,3},{4,5},{6,7},{8,9},{10,11},{12,13},{14,15},{16,17},{18,... | collective-permute-start | bytes 2168 | tf_op jit(solution)/shard_map/ppermute | solution.py:23
  402.4 39.6 %all-reduce = (f32[]{:T(128)}, f32[]{:T(128)}) all-reduce(f32[]{:T(128)} %get-tuple-element.79, f32[]{:T(128)} %get-tuple-element.78), channel_id=1, replica_groups=mesh['gx'=4,'gy'=4,'gz'=2] {'gx','gy','gz'}, use_global_device_ids=true, to_apply=%region_9.10 | all-reduce | flops 2 | bytes 16 | tf_op jit(solution)/shard_map/psum | solution.py:80
  (258 shorter events, 260.0 us)
Async XLA Ops:
  22.3 8.1 %collective-permute-start.4 = (f32[10,18,1]{2,1,0:T(8,128)S(1)}, f32[10,18,1]{2,1,0:T(8,128)S(1)}, u32[]{:S(2)}, u32[]{:S(2)}) collective-permute-start(f32[10,18,1]{2,1,0:T(8,128)S(1)} %get-tuple-element.100), channel_id=1, source_target_pairs={{1,0},{3,2},{5,4},{7,6},{9,8},{11,10},{13,12},{15,14},{17,16},{19,... | collective-permute-start | bytes 2168 | tf_op jit(solution)/shard_map/ppermute | solution.py:25
  23.6 8.0 %collective-permute-start.5 = (f32[10,18,1]{2,1,0:T(8,128)S(1)}, f32[10,18,1]{2,1,0:T(8,128)S(1)}, u32[]{:S(2)}, u32[]{:S(2)}) collective-permute-start(f32[10,18,1]{2,1,0:T(8,128)S(1)} %get-tuple-element.101), channel_id=1, source_target_pairs={{0,1},{2,3},{4,5},{6,7},{8,9},{10,11},{12,13},{14,15},{16,17},{18,... | collective-permute-start | bytes 2168 | tf_op jit(solution)/shard_map/ppermute | solution.py:23
  54.8 6.5 %collective-permute-start.10 = (f32[6,10,1]{2,1,0:T(8,128)S(1)}, f32[6,10,1]{2,1,0:T(8,128)S(1)}, u32[]{:S(2)}, u32[]{:S(2)}) collective-permute-start(f32[6,10,1]{2,1,0:T(8,128)S(1)} %get-tuple-element.132), channel_id=1, source_target_pairs={{1,0},{3,2},{5,4},{7,6},{9,8},{11,10},{13,12},{15,14},{17,16},{19,... | collective-permute-start | bytes 728 | tf_op jit(solution)/shard_map/ppermute | solution.py:25
  56.1 6.4 %collective-permute-start.11 = (f32[6,10,1]{2,1,0:T(8,128)S(1)}, f32[6,10,1]{2,1,0:T(8,128)S(1)}, u32[]{:S(2)}, u32[]{:S(2)}) collective-permute-start(f32[6,10,1]{2,1,0:T(8,128)S(1)} %get-tuple-element.133), channel_id=1, source_target_pairs={{0,1},{2,3},{4,5},{6,7},{8,9},{10,11},{12,13},{14,15},{16,17},{18,... | collective-permute-start | bytes 728 | tf_op jit(solution)/shard_map/ppermute | solution.py:23
  80.4 6.0 %collective-permute-start.17 = (f32[4,6,1]{2,1,0:T(8,128)S(1)}, f32[4,6,1]{2,1,0:T(8,128)S(1)}, u32[]{:S(2)}, u32[]{:S(2)}) collective-permute-start(f32[4,6,1]{2,1,0:T(8,128)S(1)} %get-tuple-element.155), channel_id=1, source_target_pairs={{0,1},{2,3},{4,5},{6,7},{8,9},{10,11},{12,13},{14,15},{16,17},{18,... | collective-permute-start | bytes 296 | tf_op jit(solution)/shard_map/ppermute | solution.py:23
  102.2 6.0 %collective-permute-start.23 = (f32[4,6,1]{2,1,0:T(8,128)S(1)}, f32[4,6,1]{2,1,0:T(8,128)S(1)}, u32[]{:S(2)}, u32[]{:S(2)}) collective-permute-start(f32[4,6,1]{2,1,0:T(8,128)S(1)} %get-tuple-element.153), channel_id=1, source_target_pairs={{0,1},{2,3},{4,5},{6,7},{8,9},{10,11},{12,13},{14,15},{16,17},{18,... | collective-permute-start | bytes 296 | tf_op jit(solution)/shard_map/ppermute | solution.py:23
  123.0 6.5 %collective-permute-start.28 = (f32[6,10,1]{2,1,0:T(8,128)S(1)}, f32[6,10,1]{2,1,0:T(8,128)S(1)}, u32[]{:S(2)}, u32[]{:S(2)}) collective-permute-start(f32[6,10,1]{2,1,0:T(8,128)S(1)} %get-tuple-element.130), channel_id=1, source_target_pairs={{1,0},{3,2},{5,4},{7,6},{9,8},{11,10},{13,12},{15,14},{17,16},{19,... | collective-permute-start | bytes 728 | tf_op jit(solution)/shard_map/ppermute | solution.py:25
  124.3 6.4 %collective-permute-start.29 = (f32[6,10,1]{2,1,0:T(8,128)S(1)}, f32[6,10,1]{2,1,0:T(8,128)S(1)}, u32[]{:S(2)}, u32[]{:S(2)}) collective-permute-start(f32[6,10,1]{2,1,0:T(8,128)S(1)} %get-tuple-element.131), channel_id=1, source_target_pairs={{0,1},{2,3},{4,5},{6,7},{8,9},{10,11},{12,13},{14,15},{16,17},{18,... | collective-permute-start | bytes 728 | tf_op jit(solution)/shard_map/ppermute | solution.py:23
  151.8 8.1 %collective-permute-start.34 = (f32[10,18,1]{2,1,0:T(8,128)S(1)}, f32[10,18,1]{2,1,0:T(8,128)S(1)}, u32[]{:S(2)}, u32[]{:S(2)}) collective-permute-start(f32[10,18,1]{2,1,0:T(8,128)S(1)} %get-tuple-element.98), channel_id=1, source_target_pairs={{1,0},{3,2},{5,4},{7,6},{9,8},{11,10},{13,12},{15,14},{17,16},{19,... | collective-permute-start | bytes 2168 | tf_op jit(solution)/shard_map/ppermute | solution.py:25
  153.1 8.0 %collective-permute-start.35 = (f32[10,18,1]{2,1,0:T(8,128)S(1)}, f32[10,18,1]{2,1,0:T(8,128)S(1)}, u32[]{:S(2)}, u32[]{:S(2)}) collective-permute-start(f32[10,18,1]{2,1,0:T(8,128)S(1)} %get-tuple-element.99), channel_id=1, source_target_pairs={{0,1},{2,3},{4,5},{6,7},{8,9},{10,11},{12,13},{14,15},{16,17},{18,... | collective-permute-start | bytes 2168 | tf_op jit(solution)/shard_map/ppermute | solution.py:23
  174.8 8.0 %collective-permute-start.40 = (f32[10,18,1]{2,1,0:T(8,128)S(1)}, f32[10,18,1]{2,1,0:T(8,128)S(1)}, u32[]{:S(2)}, u32[]{:S(2)}) collective-permute-start(f32[10,18,1]{2,1,0:T(8,128)S(1)} %get-tuple-element.96), channel_id=1, source_target_pairs={{1,0},{3,2},{5,4},{7,6},{9,8},{11,10},{13,12},{15,14},{17,16},{19,... | collective-permute-start | bytes 2168 | tf_op jit(solution)/shard_map/ppermute | solution.py:25
  176.1 8.1 %collective-permute-start.41 = (f32[10,18,1]{2,1,0:T(8,128)S(1)}, f32[10,18,1]{2,1,0:T(8,128)S(1)}, u32[]{:S(2)}, u32[]{:S(2)}) collective-permute-start(f32[10,18,1]{2,1,0:T(8,128)S(1)} %get-tuple-element.97), channel_id=1, source_target_pairs={{0,1},{2,3},{4,5},{6,7},{8,9},{10,11},{12,13},{14,15},{16,17},{18,... | collective-permute-start | bytes 2168 | tf_op jit(solution)/shard_map/ppermute | solution.py:23
  242.3 8.1 %collective-permute-start.46 = (f32[10,18,1]{2,1,0:T(8,128)S(1)}, f32[10,18,1]{2,1,0:T(8,128)S(1)}, u32[]{:S(2)}, u32[]{:S(2)}) collective-permute-start(f32[10,18,1]{2,1,0:T(8,128)S(1)} %get-tuple-element.94), channel_id=1, source_target_pairs={{1,0},{3,2},{5,4},{7,6},{9,8},{11,10},{13,12},{15,14},{17,16},{19,... | collective-permute-start | bytes 2168 | tf_op jit(solution)/shard_map/ppermute | solution.py:25
  243.6 8.0 %collective-permute-start.47 = (f32[10,18,1]{2,1,0:T(8,128)S(1)}, f32[10,18,1]{2,1,0:T(8,128)S(1)}, u32[]{:S(2)}, u32[]{:S(2)}) collective-permute-start(f32[10,18,1]{2,1,0:T(8,128)S(1)} %get-tuple-element.95), channel_id=1, source_target_pairs={{0,1},{2,3},{4,5},{6,7},{8,9},{10,11},{12,13},{14,15},{16,17},{18,... | collective-permute-start | bytes 2168 | tf_op jit(solution)/shard_map/ppermute | solution.py:23
  273.9 6.5 %collective-permute-start.52 = (f32[6,10,1]{2,1,0:T(8,128)S(1)}, f32[6,10,1]{2,1,0:T(8,128)S(1)}, u32[]{:S(2)}, u32[]{:S(2)}) collective-permute-start(f32[6,10,1]{2,1,0:T(8,128)S(1)} %get-tuple-element.128), channel_id=1, source_target_pairs={{1,0},{3,2},{5,4},{7,6},{9,8},{11,10},{13,12},{15,14},{17,16},{19,... | collective-permute-start | bytes 728 | tf_op jit(solution)/shard_map/ppermute | solution.py:25
  275.2 6.4 %collective-permute-start.53 = (f32[6,10,1]{2,1,0:T(8,128)S(1)}, f32[6,10,1]{2,1,0:T(8,128)S(1)}, u32[]{:S(2)}, u32[]{:S(2)}) collective-permute-start(f32[6,10,1]{2,1,0:T(8,128)S(1)} %get-tuple-element.129), channel_id=1, source_target_pairs={{0,1},{2,3},{4,5},{6,7},{8,9},{10,11},{12,13},{14,15},{16,17},{18,... | collective-permute-start | bytes 728 | tf_op jit(solution)/shard_map/ppermute | solution.py:23
  297.9 6.0 %collective-permute-start.59 = (f32[4,6,1]{2,1,0:T(8,128)S(1)}, f32[4,6,1]{2,1,0:T(8,128)S(1)}, u32[]{:S(2)}, u32[]{:S(2)}) collective-permute-start(f32[4,6,1]{2,1,0:T(8,128)S(1)} %get-tuple-element.147), channel_id=1, source_target_pairs={{0,1},{2,3},{4,5},{6,7},{8,9},{10,11},{12,13},{14,15},{16,17},{18,... | collective-permute-start | bytes 296 | tf_op jit(solution)/shard_map/ppermute | solution.py:23
  319.6 6.0 %collective-permute-start.65 = (f32[4,6,1]{2,1,0:T(8,128)S(1)}, f32[4,6,1]{2,1,0:T(8,128)S(1)}, u32[]{:S(2)}, u32[]{:S(2)}) collective-permute-start(f32[4,6,1]{2,1,0:T(8,128)S(1)} %get-tuple-element.145), channel_id=1, source_target_pairs={{0,1},{2,3},{4,5},{6,7},{8,9},{10,11},{12,13},{14,15},{16,17},{18,... | collective-permute-start | bytes 296 | tf_op jit(solution)/shard_map/ppermute | solution.py:23
  340.5 6.5 %collective-permute-start.70 = (f32[6,10,1]{2,1,0:T(8,128)S(1)}, f32[6,10,1]{2,1,0:T(8,128)S(1)}, u32[]{:S(2)}, u32[]{:S(2)}) collective-permute-start(f32[6,10,1]{2,1,0:T(8,128)S(1)} %get-tuple-element.126), channel_id=1, source_target_pairs={{1,0},{3,2},{5,4},{7,6},{9,8},{11,10},{13,12},{15,14},{17,16},{19,... | collective-permute-start | bytes 728 | tf_op jit(solution)/shard_map/ppermute | solution.py:25
  341.8 6.4 %collective-permute-start.71 = (f32[6,10,1]{2,1,0:T(8,128)S(1)}, f32[6,10,1]{2,1,0:T(8,128)S(1)}, u32[]{:S(2)}, u32[]{:S(2)}) collective-permute-start(f32[6,10,1]{2,1,0:T(8,128)S(1)} %get-tuple-element.127), channel_id=1, source_target_pairs={{0,1},{2,3},{4,5},{6,7},{8,9},{10,11},{12,13},{14,15},{16,17},{18,... | collective-permute-start | bytes 728 | tf_op jit(solution)/shard_map/ppermute | solution.py:23
  369.3 8.1 %collective-permute-start.76 = (f32[10,18,1]{2,1,0:T(8,128)S(1)}, f32[10,18,1]{2,1,0:T(8,128)S(1)}, u32[]{:S(2)}, u32[]{:S(2)}) collective-permute-start(f32[10,18,1]{2,1,0:T(8,128)S(1)} %get-tuple-element.92), channel_id=1, source_target_pairs={{1,0},{3,2},{5,4},{7,6},{9,8},{11,10},{13,12},{15,14},{17,16},{19,... | collective-permute-start | bytes 2168 | tf_op jit(solution)/shard_map/ppermute | solution.py:25
  370.6 8.0 %collective-permute-start.77 = (f32[10,18,1]{2,1,0:T(8,128)S(1)}, f32[10,18,1]{2,1,0:T(8,128)S(1)}, u32[]{:S(2)}, u32[]{:S(2)}) collective-permute-start(f32[10,18,1]{2,1,0:T(8,128)S(1)} %get-tuple-element.93), channel_id=1, source_target_pairs={{0,1},{2,3},{4,5},{6,7},{8,9},{10,11},{12,13},{14,15},{16,17},{18,... | collective-permute-start | bytes 2168 | tf_op jit(solution)/shard_map/ppermute | solution.py:23
  392.2 8.0 %collective-permute-start.82 = (f32[10,18,1]{2,1,0:T(8,128)S(1)}, f32[10,18,1]{2,1,0:T(8,128)S(1)}, u32[]{:S(2)}, u32[]{:S(2)}) collective-permute-start(f32[10,18,1]{2,1,0:T(8,128)S(1)} %get-tuple-element.90), channel_id=1, source_target_pairs={{1,0},{3,2},{5,4},{7,6},{9,8},{11,10},{13,12},{15,14},{17,16},{19,... | collective-permute-start | bytes 2168 | tf_op jit(solution)/shard_map/ppermute | solution.py:25
  393.5 8.1 %collective-permute-start.83 = (f32[10,18,1]{2,1,0:T(8,128)S(1)}, f32[10,18,1]{2,1,0:T(8,128)S(1)}, u32[]{:S(2)}, u32[]{:S(2)}) collective-permute-start(f32[10,18,1]{2,1,0:T(8,128)S(1)} %get-tuple-element.91), channel_id=1, source_target_pairs={{0,1},{2,3},{4,5},{6,7},{8,9},{10,11},{12,13},{14,15},{16,17},{18,... | collective-permute-start | bytes 2168 | tf_op jit(solution)/shard_map/ppermute | solution.py:23
  (60 other events, 263.9 us)
where the time goes:
time: 450 us; the launch traced here: 447 us
  starting transfers between devices  177 us (39%)
  waiting for transfers between devices  142 us (32%)
  blocking collectives  79.2 us (18%)
  local copies, waits for them, and re-layouts  28.4 us (6%)
  other arithmetic  13.1 us (3%)
  between operations  7.66 us (2%)
    ppermute x42, waiting for transfers between devices, padded_2(): lax.ppermute(head, axis, [((i + 1) % count, i) for i in range(ends)])  124 us
    ppermute x42, starting transfers between devices, padded_2(): lax.ppermute(tail, axis, [(i, (i + 1) % count) for i in range(ends)])  122 us
    psum x2, blocking collectives, joint_sums(): lax.psum((jnp.sum(residual * precond), jnp.sum(precond * precond_image)),...  79.2 us
    ppermute x42, starting transfers between devices, padded_2(): lax.ppermute(head, axis, [((i + 1) % count, i) for i in range(ends)])  54.2 us
    ppermute x42, waiting for transfers between devices, padded_2(): lax.ppermute(tail, axis, [(i, (i + 1) % count) for i in range(ends)])  18.2 us
    reshape x4, local copies, waits for them, and re-layouts, restrict(): field.reshape(sx // 2, 2, sy // 2, 2, sz // 2, 2)  12.1 us
  transfers between devices with their start and end apart: 84, of which 52 were waited for; matrix products, arithmetic and copies ran while one was open for 0% of the time, Pallas kernels for 0%

commit v1 on v0

v1 whole, which is shorter than its diff:
```python
import functools

import jax
import jax.numpy as jnp
from jax import lax
from jax.experimental import pallas as pl
from jax.experimental.pallas import tpu as pltpu
from jax.sharding import PartitionSpec as P

W = 1.0 / 9.0
COUPLING = 0.5
MESH = pl.DeviceIdType.MESH
REACH = 7


def lane_of(shape):
    return lax.broadcasted_iota(jnp.int32, shape, len(shape) - 1)


def roll(x, shift, axis):
    return pltpu.roll(x, shift % x.shape[axis], axis)


def kernel(
    ns, bx, by, bz, kx, ky,
    den, xf, yf, zf, sol, res,
    fld, ysrc, yrec, zsrc, zrec, tmp, prol, dsrc, win, sums,
    fsend, frecv, dsend, drecv, ssend, srecv, *rest,
):
    nx, ny, nz = ns
    gx, gy, gz = (lax.axis_index(a) for a in ("gx", "gy", "gz"))
    hx, hy, hz = bx // 2, by // 2, bz // 2
    me = (gx * ny + gy) * nz + gz
    total = nx * ny * nz
    f32 = jnp.float32

    fld[...] = jnp.zeros_like(fld)
    yrec[...] = jnp.zeros_like(yrec)
    zrec[...] = jnp.zeros_like(zrec)
    win[...] = jnp.zeros_like(win)

    barrier = pltpu.get_barrier_semaphore()

    def coords(flat):
        return (flat // (ny * nz), lax.rem(flat // nz, ny), lax.rem(flat, nz))

    def greet(step, c):
        other = lax.rem(me + step, total)
        pl.semaphore_signal(barrier, inc=1, device_id=coords(other), device_id_type=MESH)
        return c

    lax.fori_loop(1, total, greet, 0)

    lane = lane_of((by, bz))
    eye = lax.broadcasted_iota(jnp.int32, (by, by), 0) == lax.broadcasted_iota(jnp.int32, (by, by), 1)
    row = lax.broadcasted_iota(jnp.int32, (by, bz), 0)
    planes = []
    for p in range(bx):
        r = -COUPLING * den[p]
        if p == 0:
            r = r + jnp.where(gx == 0, xf[0], 0.0)
        if p == bx - 1:
            r = r + jnp.where(gx == nx - 1, xf[1], 0.0)
        r = r + jnp.where((row == 0) & (gy == 0), yf[0, p : p + 1, :], 0.0)
        r = r + jnp.where((row == by - 1) & (gy == ny - 1), yf[1, p : p + 1, :], 0.0)
        for side, (at, edge) in enumerate(((0, 0), (bz - 1, nz - 1))):
            col = jnp.sum(jnp.where(eye, zf[side, p : p + 1, :], 0.0), axis=1, keepdims=True)
            r = r + jnp.where((lane == at) & (gz == edge), col, 0.0)
        planes.append(r)
    r0 = jnp.stack(planes)

    pl.semaphore_wait(barrier, total - 1)

    def pack(field, at, rep):
        out = jnp.zeros((by, bz), f32)
        for p in range(bx):
            out = jnp.where(lane == p, roll(field[p // rep], p - at, 1), out)
        return out

    def faces(k, do):
        def one(s, src, dst, dev, there, back):
            if do == "start":
                @pl.when(there)
                def _():
                    pltpu.make_async_remote_copy(
                        src, dst, fsend.at[k, s], frecv.at[k, s], device_id=dev, device_id_type=MESH
                    ).start()
            else:
                @pl.when(there)
                def _():
                    pltpu.make_async_remote_copy(
                        src, dst, fsend.at[k, s], frecv.at[k, s], device_id=dev, device_id_type=MESH
                    ).wait_send()

                @pl.when(back)
                def _():
                    pltpu.make_async_remote_copy(
                        src, dst, fsend.at[k, s], frecv.at[k, s], device_id=dev, device_id_type=MESH
                    ).wait_recv()

        own = pl.ds(8, by)
        xl, xr, yl, yr, zl, zr = gx > 0, gx < nx - 1, gy > 0, gy < ny - 1, gz > 0, gz < nz - 1
        one(0, fld.at[k, bx, own], fld.at[k, 0, own], (gx + 1, gy, gz), xr, xl)
        one(1, fld.at[k, 1, own], fld.at[k, bx + 1, own], (gx - 1, gy, gz), xl, xr)
        one(2, ysrc.at[k, 1], yrec.at[k, 0], (gx, gy + 1, gz), yr, yl)
        one(3, ysrc.at[k, 0], yrec.at[k, 1], (gx, gy - 1, gz), yl, yr)
        one(4, zsrc.at[k, 1], zrec.at[k, 0], (gx, gy, gz + 1), zr, zl)
        one(5, zsrc.at[k, 0], zrec.at[k, 1], (gx, gy, gz - 1), zl, zr)

    def exchange(k, value):
        fld[k, 1 : bx + 1, 8 : 8 + by, :] = value
        for p in range(bx):
            ysrc[k, 0, p : p + 1, :] = value[p, 0:1, :]
            ysrc[k, 1, p : p + 1, :] = value[p, by - 1 : by, :]
        zsrc[k, 0] = pack(value, 0, 1)
        zsrc[k, 1] = pack(value, bz - 1, 1)
        faces(k, "start")
        faces(k, "wait")
        for p in range(bx):
            fld[k, p + 1, 7:8, :] = yrec[k, 0, p : p + 1, :]
            fld[k, p + 1, 8 + by : 9 + by, :] = yrec[k, 1, p : p + 1, :]

    def operate(ref, zl, zr):
        out = []
        for p in range(bx):
            c = ref[p + 1, 8 : 8 + by, :]
            s = ref[p, 8 : 8 + by, :] + ref[p + 2, 8 : 8 + by, :]
            s = s + ref[p + 1, 7 : 7 + by, :] + ref[p + 1, 9 : 9 + by, :]
            s = s + jnp.where(lane == 0, roll(zl, -p, 1), roll(c, 1, 1))
            s = s + jnp.where(lane == bz - 1, roll(zr, bz - 1 - p, 1), roll(c, -1, 1))
            out.append(6.0 * c - s)
        return jnp.stack(out)

    offsets = [
        (dx, dy, dz)
        for dx in range(-kx, kx + 1) for dy in range(-ky, ky + 1) for dz in (-1, 0, 1)
        if (dx, dy, dz) != (0, 0, 0) and abs(dx) < nx and abs(dy) < ny and abs(dz) < nz
    ]

    def gather(c, do):
        for dx, dy, dz in offsets:
            def copy(dx=dx, dy=dy, dz=dz):
                i = ((dx + kx) * (2 * ky + 1) + dy + ky) * 3 + dz + 1
                return pltpu.make_async_remote_copy(
                    dsrc.at[c],
                    win.at[c, 1 - dz, pl.ds((kx - dx) * hx, hx), pl.ds((ky - dy) * hy, hy)],
                    dsend.at[c, i], drecv.at[c, i],
                    device_id=(gx + dx, gy + dy, gz + dz), device_id_type=MESH,
                )

            def there(s):
                x, y, z = gx + s * dx, gy + s * dy, gz + s * dz
                return (x >= 0) & (x < nx) & (y >= 0) & (y < ny) & (z >= 0) & (z < nz)

            if do == "start":
                @pl.when(there(1))
                def _():
                    copy().start()
            else:
                @pl.when(there(1))
                def _():
                    copy().wait_send()

                @pl.when(there(-1))
                def _():
                    copy().wait_recv()

    wx, wy = (2 * kx + 1) * hx, (2 * ky + 1) * hy
    ex = kx * hx
    ey = ky * hy
    q = bz // 4

    def dims(n0, n1, half):
        shape = (n1 - n0, wy, bz)
        x = lax.broadcasted_iota(jnp.int32, shape, 0) + n0
        y = lax.broadcasted_iota(jnp.int32, shape, 1)
        z = lax.broadcasted_iota(jnp.int32, shape, 2)
        x = x + (gx * hx - ex) // half
        y = y + gy * hy - ey
        z = z + gz * hz - q
        return (
            (x >= 0) & (x < nx * hx // half) & (y >= 0) & (y < ny * hy) & (z >= 0) & (z < nz * hz)
        )

    def beside(v, step):
        m = v[1:-1]
        s = v[:-2] + v[2:]
        s = s + roll(m, step, 1) + roll(m, -step, 1)
        return s + roll(m, step, 2) + roll(m, -step, 2)

    def twin(v, axis):
        even = lax.broadcasted_iota(jnp.int32, v.shape, axis) % 2 == 0
        return v + jnp.where(even, roll(v, -1, axis), roll(v, 1, axis))

    def coarse(c):
        a0, a1 = ex - REACH, ex + hx + REACH
        zi = lane_of((a1 - a0, wy, bz))
        d = jnp.where(zi < q, win[c, 0, a0:a1], jnp.where(zi < q + hz, win[c, 1, a0:a1], win[c, 2, a0:a1]))
        v = W * d
        defect = d[1:-1] - (6.0 * v[1:-1] - beside(v, 1))
        n = defect.shape[0] // 2
        defect = defect.reshape(n, 2, wy, bz)
        r = 0.5 * twin(twin(defect[:, 0] + defect[:, 1], 1), 2)
        b0 = (a0 + 1) // 2
        m2 = dims(b0, b0 + n, 2)
        r = jnp.where(m2, r, 0.0)
        e = W * r
        e = jnp.where(m2[1:-1], e[1:-1] + W * (r[1:-1] - (6.0 * e[1:-1] - beside(e, 2))), 0.0)
        r = r[2:-2]
        e = jnp.where(m2[2:-2], e[1:-1] + W * (r - (6.0 * e[1:-1] - beside(e, 2))), 0.0)
        k0 = (b0 + 2) * 2 - a0
        spread = jnp.stack([e, e], axis=1).reshape(2 * e.shape[0], wy, bz)
        d = d[k0 : k0 + spread.shape[0]]
        v = W * d + spread
        out = v[1:-1] + W * (d[1:-1] - (6.0 * v[1:-1] - beside(v, 1)))
        p0 = (b0 + 2) * 2 + 1
        return jnp.where(dims(p0, p0 + out.shape[0], 1), out, 0.0), p0

    li = lax.broadcasted_iota(jnp.int32, (bz, bz), 0)
    lj = lax.broadcasted_iota(jnp.int32, (bz, bz), 1)
    shrink = jnp.where(li // 2 == (lj - q + hz) % hz, 0.5, 0.0).astype(f32)
    grow = jnp.where(li == q + lj // 2, 1.0, 0.0).astype(f32)
    dot = functools.partial(jnp.dot, precision=lax.Precision.HIGHEST, preferred_element_type=f32)

    def cycle_and_image(c, r):
        k = 2 * c
        exchange(k, r)
        rref = fld.at[k]
        rzl, rzr = zrec[k, 0], zrec[k, 1]
        defect = r - W * operate(rref, rzl, rzr)
        defect = defect.reshape(hx, 2, by, bz)
        tmp[...] = defect[:, 0] + defect[:, 1]
        half = tmp[:, pl.ds(0, hy, stride=2), :] + tmp[:, pl.ds(1, hy, stride=2), :]
        d1 = dot(half.reshape(hx * hy, bz), shrink).reshape(hx, hy, bz)
        dsrc[c] = d1
        win[c, 1, ex : ex + hx, ey : ey + hy, :] = d1
        gather(c, "start")
        gather(c, "wait")
        e1, p0 = coarse(c)
        e1 = e1[ex - 1 - p0 : ex + hx + 1 - p0, ey - 4 : ey + hy + 4]
        n = hy + 8
        prol[:, pl.ds(0, n, stride=2), :] = e1
        prol[:, pl.ds(1, n, stride=2), :] = e1
        own = prol[1 : hx + 1, 8 : 8 + by, :]
        vzl = W * rzl + pack(own, q - 1, 2)
        vzr = W * rzr + pack(own, q + hz, 2)
        fine = dot(prol[...].reshape((hx + 2) * 2 * n, bz), grow).reshape(hx + 2, 2 * n, bz)
        v = rest[0]
        for i in range(bx + 2):
            v[i] = W * rref[i] + fine[1 + (i - 1) // 2]
        z = v[1 : bx + 1, 8 : 8 + by, :] + W * (r - operate(v, vzl, vzr))
        exchange(k + 1, z)
        return z, operate(fld.at[k + 1], zrec[k + 1, 0], zrec[k + 1, 1])

    z0, w = cycle_and_image(0, r0)
    u, aw = cycle_and_image(1, w)

    pairs = ((r0, z0), (z0, w), (r0, u), (w, u), (u, aw), (z0, aw))
    l1 = lane_of((1, bz))
    mine = jnp.zeros((1, bz), f32)
    for i, (a, b) in enumerate(pairs):
        s = jnp.sum(jnp.sum(jnp.sum(a * b, axis=0), axis=0, keepdims=True), axis=1, keepdims=True)
        mine = jnp.where(l1 == i, s, mine)
    sums[me] = mine

    def share(do):
        def step(i, carry):
            other = lax.rem(me + i, total)
            source = lax.rem(me + total - i, total)
            if do == "start":
                pltpu.make_async_remote_copy(
                    sums.at[me], sums.at[me], ssend.at[i], srecv.at[i],
                    device_id=coords(other), device_id_type=MESH,
                ).start()
            else:
                pltpu.make_async_remote_copy(
                    sums.at[me], sums.at[source], ssend.at[i], srecv.at[i],
                    device_id=coords(other), device_id_type=MESH,
                ).wait()
            return carry

        lax.fori_loop(1, total, step, 0)

    share("start")
    share("wait")
    tot = jnp.sum(sums[...], axis=0)

    def scalar(i):
        return jnp.sum(jnp.where(l1 == i, tot, 0.0), axis=1, keepdims=True)

    g0, d0, ru, wu, uv, zv = (scalar(i) for i in range(6))
    a = g0 / d0
    g1 = (g0 - a * d0) - a * ru + a * a * wu
    beta = g1 / g0
    zaz = d0 - a * (wu + zv) + a * a * uv
    cross = (d0 - a * wu) + (d0 - a * zv)
    b = g1 / (zaz + beta * cross + beta * beta * d0)
    for p in range(bx):
        d1 = (z0[p] - a * u[p]) + beta * z0[p]
        i1 = (w[p] - a * aw[p]) + beta * w[p]
        sol[p] = a * z0[p] + b * d1
        res[p] = (r0[p] - a * w[p]) - b * i1


def solution(mesh):
    ns = tuple(mesh.shape[a] for a in ("gx", "gy", "gz"))

    def local(density, x_faces, y_faces, z_faces):
        bx, by, bz = density.shape
        kx = min(-(-REACH // (bx // 2)), 10**6)
        ky = -(-REACH // (by // 2))
        hx, hy = bx // 2, by // 2
        vm = pl.BlockSpec(memory_space=pltpu.VMEM)
        total = ns[0] * ns[1] * ns[2]
        near = (2 * kx + 1) * (2 * ky + 1) * 3
        f32 = jnp.float32
        dma = pltpu.SemaphoreType.DMA
        return pl.pallas_call(
            functools.partial(kernel, ns, bx, by, bz, kx, ky),
            out_shape=(jax.ShapeDtypeStruct(density.shape, f32),) * 2,
            in_specs=[vm] * 4,
            out_specs=(vm, vm),
            scratch_shapes=[
                pltpu.VMEM((4, bx + 2, by + 16, bz), f32),
                pltpu.VMEM((4, 2, bx, bz), f32),
                pltpu.VMEM((4, 2, bx, bz), f32),
                pltpu.VMEM((4, 2, by, bz), f32),
                pltpu.VMEM((4, 2, by, bz), f32),
                pltpu.VMEM((hx, by, bz), f32),
                pltpu.VMEM((hx + 2, by + 16, bz), f32),
                pltpu.VMEM((2, hx, hy, bz), f32),
                pltpu.VMEM((2, 3, (2 * kx + 1) * hx, (2 * ky + 1) * hy, bz), f32),
                pltpu.VMEM((total, 1, bz), f32),
                dma((4, 6)),
                dma((4, 6)),
                dma((2, near)),
                dma((2, near)),
                dma((total,)),
                dma((total,)),
                pltpu.VMEM((bx + 2, by + 16, bz), f32),
            ],
            compiler_params=pltpu.CompilerParams(collective_id=0, has_side_effects=True),
        )(density, x_faces, y_faces, z_faces)

    return jax.shard_map(
        local,
        mesh=mesh,
        in_specs=(P("gx", "gy", "gz"), P(None, "gy", "gz"), P(None, "gx", "gz"), P(None, "gx", "gy")),
        out_specs=(P("gx", "gy", "gz"), P("gx", "gy", "gz")),
        check_vma=False,
    )
```

time: 450 us -> 43.4 us (0.10)
  starting transfers between devices: 177 us -> 0 us
  waiting for transfers between devices: 142 us -> 0 us
  blocking collectives: 79.2 us -> 0 us
  Pallas kernels: 0 us -> 40.4 us
  local copies, waits for them, and re-layouts: 28.4 us -> 2.14 us
  other arithmetic: 13.1 us -> 0 us
  between operations: 7.66 us -> 0.65 us
    ppermute x84 -> x0, starting transfers between devices: 177 us -> none  [the longest x42 122 us: padded_2(): lax.ppermute(tail, axis, [(i, (i + 1) % count) for i in range(ends)])]
    ppermute x84 -> x0, waiting for transfers between devices: 142 us -> none  [the longest x42 124 us: padded_2(): lax.ppermute(head, axis, [((i + 1) % count, i) for i in range(ends)])]
    psum x2 -> x0, blocking collectives: 79.2 us -> none  [joint_sums(): lax.psum((jnp.sum(residual * precond), jnp.sum(precond * precond_image)),...]
    pallas_call x0 -> x1, Pallas kernels: none -> 40.4 us  [local(): pl.pallas_call(functools.partial(kernel, ns, bx, by, bz, kx, ky), out_sha...]
    reshape x8 -> x0, local copies, waits for them, and re-layouts: 20.7 us -> none  [the longest x4 12.1 us: restrict(): field.reshape(sx // 2, 2, sy // 2, 2, sz // 2, 2)]
    reduce_sum x6 -> x0, other arithmetic: 6.88 us -> none  [the longest x4 5.33 us: restrict(): jnp.sum(field.reshape(sx // 2, 2, sy // 2, 2, sz // 2, 2), axis=(1, 3, 5))]
    broadcast_in_dim x4 -> x0, local copies, waits for them, and re-layouts: 5.44 us -> none  [prolong(): jnp.broadcast_to(field[:, None, :, None, :, None], (sx, 2, sy, 2, sz, 2))]
  transfers between devices with their start and end apart: 84 -> 0, of which waited for: 52 -> 0; matrix products, arithmetic and copies ran while one was open for 0% -> 0% of each run, Pallas kernels for 0% -> 0%
where the time goes in v1:
time: 43.4 us; the launch traced here: 43.1 us
  Pallas kernels  40.4 us (93%)
  local copies, waits for them, and re-layouts  2.14 us (5%)
  between operations  0.65 us (1%)
    pallas_call x1, Pallas kernels, local(): pl.pallas_call(functools.partial(kernel, ns, bx, by, bz, kx, ky), out_sha...  40.4 us
    unnamed x4, local copies, waits for them, and re-layouts  2.14 us

profile of v1, /device:TPU:0, one launch (start us, length us, event | category | flops | bytes accessed | tf_op | source)
XLA Modules:
  0.0 43.1 jit_solution(11488288379079404444)
XLA Ops:
  0.6 40.4 %shard_map.59 = (f32[8,16,128]{2,1,0:T(8,128)}, f32[8,16,128]{2,1,0:T(8,128)}) custom-call(f32[8,16,128]{2,1,0:T(8,128)} %den.1, f32[2,16,128]{2,1,0:T(8,128)} %xf.1, f32[2,8,128]{2,1,0:T(8,128)} %yf.1, f32[2,8,16]{2,1,0:T(8,128)} %zf.1), custom_call_target="tpu_custom_call" | custom-call | tf_op jit(solution)/shard_map/pallas_call | solution.py:318
  41.0 0.0 copy-start
  41.0 1.5 %copy.8 = f32[8,16,128]{2,1,0:T(8,128)} copy(f32[8,16,128]{2,1,0:T(8,128)} %get-tuple-element.4) | data formatting | bytes 131072
  42.5 0.0 copy-done
  42.5 0.6 %copy.9 = f32[8,16,128]{2,1,0:T(8,128)} copy(f32[8,16,128]{2,1,0:T(8,128)S(1)} %copy-done) | data formatting | bytes 131072
Async XLA Ops:
  41.0 1.5 %copy-start = (f32[8,16,128]{2,1,0:T(8,128)S(1)}, f32[8,16,128]{2,1,0:T(8,128)}, u32[]{:S(2)}) copy-start(f32[8,16,128]{2,1,0:T(8,128)} %get-tuple-element.5) | copy-start | bytes 196612

commit v2 on v1

--- a/solution.py
+++ b/solution.py
@@ -25,7 +25,8 @@
     ns, bx, by, bz, kx, ky,
     den, xf, yf, zf, sol, res,
     fld, ysrc, yrec, zsrc, zrec, tmp, prol, dsrc, win, sums,
-    fsend, frecv, dsend, drecv, ssend, srecv, *rest,
+    fsend, frecv, dsend, drecv, ssend, srecv,
+    xyrec, pk, vfld, vpk, zfld, zpk,
 ):
     nx, ny, nz = ns
     gx, gy, gz = (lax.axis_index(a) for a in ("gx", "gy", "gz"))
@@ -38,6 +39,8 @@
     yrec[...] = jnp.zeros_like(yrec)
     zrec[...] = jnp.zeros_like(zrec)
     win[...] = jnp.zeros_like(win)
+    xyrec[...] = jnp.zeros_like(xyrec)
+    pk[...] = jnp.zeros_like(pk)
 
     barrier = pltpu.get_barrier_semaphore()
 
@@ -71,65 +74,105 @@
 
     pl.semaphore_wait(barrier, total - 1)
 
-    def pack(field, at, rep):
-        out = jnp.zeros((by, bz), f32)
+    lane8 = lane_of((8, bz))
+    lanef = lane_of((by + 16, bz))
+    halves = by // 8
+    own = pl.ds(8, by)
+
+    def exists(x, y, z):
+        return (x >= 0) & (x < nx) & (y >= 0) & (y < ny) & (z >= 0) & (z < nz)
+
+    def transfer(items, do):
+        for (dx, dy, dz), src, dst, ss, rs in items:
+            def copy(src=src, dst=dst, ss=ss, rs=rs, to=(gx + dx, gy + dy, gz + dz)):
+                return pltpu.make_async_remote_copy(
+                    src, dst, ss, rs, device_id=to, device_id_type=MESH
+                )
+
+            if do == "start":
+                @pl.when(exists(gx + dx, gy + dy, gz + dz))
+                def _():
+                    copy().start()
+            elif do == "sent":
+                @pl.when(exists(gx + dx, gy + dy, gz + dz))
+                def _():
+                    copy().wait_send()
+            else:
+                @pl.when(exists(gx - dx, gy - dy, gz - dz))
+                def _():
+                    copy().wait_recv()
+
+    def messages(c):
+        f = fld.at[c]
+        raw = [
+            ((1, 0, 0), f.at[bx : bx + 2, own], f.at[0:2, own]),
+            ((-1, 0, 0), f.at[2:4, own], f.at[bx + 2 : bx + 4, own]),
+            ((0, 1, 0), ysrc.at[c, 1], yrec.at[c, 0]),
+            ((0, -1, 0), ysrc.at[c, 0], yrec.at[c, 1]),
+        ]
+        for dz in (1, -1):
+            src, side = zsrc.at[c, (dz + 1) // 2], (1 - dz) // 2
+            raw.append(((0, 0, dz), src, zrec.at[c, side, 0]))
+            raw.append(((1, 0, dz), src, zrec.at[c, side, 1]))
+            raw.append(((-1, 0, dz), src, zrec.at[c, side, 2]))
+            raw.append(((0, 1, dz), src, zrec.at[c, side, 3]))
+            raw.append(((0, -1, dz), src, zrec.at[c, side, 4]))
+        for dx in (1, -1):
+            for dy in (1, -1):
+                i = (1 - dx) + (1 - dy) // 2
+                raw.append(((dx, dy, 0), ysrc.at[c, (dy + 1) // 2, 0], xyrec.at[c, i]))
+        return [
+            (o, src, dst, fsend.at[c, i], frecv.at[c, i])
+            for i, (o, src, dst) in enumerate(raw)
+            if abs(o[0]) < nx and abs(o[1]) < ny and abs(o[2]) < nz
+        ]
+
+    def exchange(c, value):
+        fld[c, 2 : bx + 2, 8 : 8 + by, :] = value
         for p in range(bx):
-            out = jnp.where(lane == p, roll(field[p // rep], p - at, 1), out)
-        return out
-
-    def faces(k, do):
-        def one(s, src, dst, dev, there, back):
-            if do == "start":
-                @pl.when(there)
-                def _():
-                    pltpu.make_async_remote_copy(
-                        src, dst, fsend.at[k, s], frecv.at[k, s], device_id=dev, device_id_type=MESH
-                    ).start()
-            else:
-                @pl.when(there)
-                def _():
-                    pltpu.make_async_remote_copy(
-                        src, dst, fsend.at[k, s], frecv.at[k, s], device_id=dev, device_id_type=MESH
-                    ).wait_send()
-
-                @pl.when(back)
-                def _():
-                    pltpu.make_async_remote_copy(
-                        src, dst, fsend.at[k, s], frecv.at[k, s], device_id=dev, device_id_type=MESH
-                    ).wait_recv()
-
-        own = pl.ds(8, by)
-        xl, xr, yl, yr, zl, zr = gx > 0, gx < nx - 1, gy > 0, gy < ny - 1, gz > 0, gz < nz - 1
-        one(0, fld.at[k, bx, own], fld.at[k, 0, own], (gx + 1, gy, gz), xr, xl)
-        one(1, fld.at[k, 1, own], fld.at[k, bx + 1, own], (gx - 1, gy, gz), xl, xr)
-        one(2, ysrc.at[k, 1], yrec.at[k, 0], (gx, gy + 1, gz), yr, yl)
-        one(3, ysrc.at[k, 0], yrec.at[k, 1], (gx, gy - 1, gz), yl, yr)
-        one(4, zsrc.at[k, 1], zrec.at[k, 0], (gx, gy, gz + 1), zr, zl)
-        one(5, zsrc.at[k, 0], zrec.at[k, 1], (gx, gy, gz - 1), zl, zr)
-
-    def exchange(k, value):
-        fld[k, 1 : bx + 1, 8 : 8 + by, :] = value
+            for d in (0, 1):
+                ysrc[c, 0, d, p : p + 1, :] = value[p, d : d + 1, :]
+                ysrc[c, 1, d, p : p + 1, :] = value[p, by - 1 - d : by - d, :]
+        for side, at in ((0, 0), (1, bz - 2)):
+            out = jnp.zeros((8, bz), f32)
+            for h in range(halves):
+                for p in range(bx):
+                    to = 2 * (h * bx + p)
+                    moved = roll(value[p, 8 * h : 8 * h + 8, :], to - at, 1)
+                    out = jnp.where(lane8 // 2 == to // 2, moved, out)
+            zsrc[c, side] = out
+        items = messages(c)
+        transfer(items, "start")
+        transfer(items, "here")
         for p in range(bx):
-            ysrc[k, 0, p : p + 1, :] = value[p, 0:1, :]
-            ysrc[k, 1, p : p + 1, :] = value[p, by - 1 : by, :]
-        zsrc[k, 0] = pack(value, 0, 1)
-        zsrc[k, 1] = pack(value, bz - 1, 1)
-        faces(k, "start")
-        faces(k, "wait")
-        for p in range(bx):
-            fld[k, p + 1, 7:8, :] = yrec[k, 0, p : p + 1, :]
-            fld[k, p + 1, 8 + by : 9 + by, :] = yrec[k, 1, p : p + 1, :]
-
-    def operate(ref, zl, zr):
-        out = []
-        for p in range(bx):
-            c = ref[p + 1, 8 : 8 + by, :]
-            s = ref[p, 8 : 8 + by, :] + ref[p + 2, 8 : 8 + by, :]
-            s = s + ref[p + 1, 7 : 7 + by, :] + ref[p + 1, 9 : 9 + by, :]
-            s = s + jnp.where(lane == 0, roll(zl, -p, 1), roll(c, 1, 1))
-            s = s + jnp.where(lane == bz - 1, roll(zr, bz - 1 - p, 1), roll(c, -1, 1))
-            out.append(6.0 * c - s)
-        return jnp.stack(out)
+            for d in (0, 1):
+                fld[c, p + 2, 7 - d : 8 - d, :] = yrec[c, 0, d, p : p + 1, :]
+                fld[c, p + 2, 8 + by + d : 9 + by + d, :] = yrec[c, 1, d, p : p + 1, :]
+        for i in range(4):
+            plane, p = ((1, bx - 1), (bx + 2, 0))[i // 2]
+            at = (7, 8 + by)[i % 2]
+            fld[c, plane, at : at + 1, :] = xyrec[c, i, p : p + 1, :]
+        for side in (0, 1):
+            t = [zrec[c, side, i] for i in range(5)]
+            for h in range(halves):
+                o = jnp.where((lane8 >= 4) & (lane8 < 4 + 2 * bx), roll(t[0], 4 - 2 * bx * h, 1), 0.0)
+                o = jnp.where(lane8 // 2 == 1, roll(t[1], 2 - 2 * (bx * h + bx - 1), 1), o)
+                o = jnp.where(lane8 // 2 == bx + 2, roll(t[2], 2 * (bx + 2) - 2 * bx * h, 1), o)
+                pk[c, side, 8 + 8 * h : 16 + 8 * h, :] = o
+            inner = (lane8 >= 4) & (lane8 < 4 + 2 * bx)
+            before = jnp.where(inner, roll(t[3], 4 - 2 * bx * (halves - 1), 1), 0.0)
+            after = jnp.where(inner, roll(t[4], 4, 1), 0.0)
+            pk[c, side, 7:8, :] = before[7:8]
+            pk[c, side, 8 + by : 9 + by, :] = after[0:1]
+
+    def operate(ref, packed, i, a, b):
+        c = ref[i, a:b, :]
+        ln = lane_of(c.shape)
+        s = ref[i - 1, a:b, :] + ref[i + 1, a:b, :]
+        s = s + ref[i, a - 1 : b - 1, :] + ref[i, a + 1 : b + 1, :]
+        s = s + jnp.where(ln == 0, packed[0, a:b, 2 * i + 1 : 2 * i + 2], roll(c, 1, 1))
+        s = s + jnp.where(ln == bz - 1, packed[1, a:b, 2 * i : 2 * i + 1], roll(c, -1, 1))
+        return 6.0 * c - s
 
     offsets = [
         (dx, dy, dz)
@@ -137,33 +180,13 @@
         if (dx, dy, dz) != (0, 0, 0) and abs(dx) < nx and abs(dy) < ny and abs(dz) < nz
     ]
 
-    def gather(c, do):
+    def gathered(c):
+        items = []
         for dx, dy, dz in offsets:
-            def copy(dx=dx, dy=dy, dz=dz):
-                i = ((dx + kx) * (2 * ky + 1) + dy + ky) * 3 + dz + 1
-                return pltpu.make_async_remote_copy(
-                    dsrc.at[c],
-                    win.at[c, 1 - dz, pl.ds((kx - dx) * hx, hx), pl.ds((ky - dy) * hy, hy)],
-                    dsend.at[c, i], drecv.at[c, i],
-                    device_id=(gx + dx, gy + dy, gz + dz), device_id_type=MESH,
-                )
-
-            def there(s):
-                x, y, z = gx + s * dx, gy + s * dy, gz + s * dz
-                return (x >= 0) & (x < nx) & (y >= 0) & (y < ny) & (z >= 0) & (z < nz)
-
-            if do == "start":
-                @pl.when(there(1))
-                def _():
-                    copy().start()
-            else:
-                @pl.when(there(1))
-                def _():
-                    copy().wait_send()
-
-                @pl.when(there(-1))
-                def _():
-                    copy().wait_recv()
+            i = ((dx + kx) * (2 * ky + 1) + dy + ky) * 3 + dz + 1
+            dst = win.at[c, 1 - dz, pl.ds((kx - dx) * hx, hx), pl.ds((ky - dy) * hy, hy)]
+            items.append(((dx, dy, dz), dsrc.at[c], dst, dsend.at[c, i], drecv.at[c, i]))
+        return items
 
     wx, wy = (2 * kx + 1) * hx, (2 * ky + 1) * hy
     ex = kx * hx
@@ -223,34 +246,52 @@
     dot = functools.partial(jnp.dot, precision=lax.Precision.HIGHEST, preferred_element_type=f32)
 
     def cycle_and_image(c, r):
-        k = 2 * c
-        exchange(k, r)
-        rref = fld.at[k]
-        rzl, rzr = zrec[k, 0], zrec[k, 1]
-        defect = r - W * operate(rref, rzl, rzr)
-        defect = defect.reshape(hx, 2, by, bz)
-        tmp[...] = defect[:, 0] + defect[:, 1]
+        exchange(c, r)
+        rref = fld.at[c]
+        for j in range(hx):
+            d = r[2 * j] + r[2 * j + 1]
+            for i in (2 * j + 2, 2 * j + 3):
+                d = d - W * operate(rref, pk.at[c], i, 8, 8 + by)
+            tmp[j] = d
         half = tmp[:, pl.ds(0, hy, stride=2), :] + tmp[:, pl.ds(1, hy, stride=2), :]
         d1 = dot(half.reshape(hx * hy, bz), shrink).reshape(hx, hy, bz)
         dsrc[c] = d1
         win[c, 1, ex : ex + hx, ey : ey + hy, :] = d1
-        gather(c, "start")
-        gather(c, "wait")
+        transfer(gathered(c), "start")
+        transfer(gathered(c), "here")
         e1, p0 = coarse(c)
         e1 = e1[ex - 1 - p0 : ex + hx + 1 - p0, ey - 4 : ey + hy + 4]
         n = hy + 8
         prol[:, pl.ds(0, n, stride=2), :] = e1
         prol[:, pl.ds(1, n, stride=2), :] = e1
-        own = prol[1 : hx + 1, 8 : 8 + by, :]
-        vzl = W * rzl + pack(own, q - 1, 2)
-        vzr = W * rzr + pack(own, q + hz, 2)
+        for side, at in ((0, q - 1), (1, q + hz)):
+            o = W * pk[c, side]
+            for j in range(hx + 2):
+                o = o + jnp.where(lanef // 4 == j, prol[j, :, at : at + 1], 0.0)
+            vpk[side] = o
         fine = dot(prol[...].reshape((hx + 2) * 2 * n, bz), grow).reshape(hx + 2, 2 * n, bz)
-        v = rest[0]
-        for i in range(bx + 2):
-            v[i] = W * rref[i] + fine[1 + (i - 1) // 2]
-        z = v[1 : bx + 1, 8 : 8 + by, :] + W * (r - operate(v, vzl, vzr))
-        exchange(k + 1, z)
-        return z, operate(fld.at[k + 1], zrec[k + 1, 0], zrec[k + 1, 1])
+        for i in range(bx + 4):
+            vfld[i] = W * rref[i] + fine[i // 2]
+        for i in range(1, bx + 3):
+            a, b = 7, 9 + by
+            z = vfld[i, a:b, :] + W * (rref[i, a:b, :] - operate(vfld, vpk, i, a, b))
+            zrow = lax.broadcasted_iota(jnp.int32, z.shape, 0)
+            inside = ((zrow > 0) | (gy > 0)) & ((zrow < by + 1) | (gy < ny - 1))
+            if i == 1:
+                inside = inside & (gx > 0)
+            if i == bx + 2:
+                inside = inside & (gx < nx - 1)
+            zfld[i, a:b, :] = jnp.where(inside, z, 0.0)
+        for side, at in ((0, 0), (1, bz - 1)):
+            o = vpk[side]
+            s = roll(o, 2, 1) + roll(o, -2, 1) + roll(o, 1, 0) + roll(o, -1, 0)
+            s = s + roll(o, 1 - 2 * side, 1)
+            for i in range(2, bx + 2):
+                s = s + jnp.where(lanef == 2 * i + 1 - side, vfld[i, :, at : at + 1], 0.0)
+            inside = gz < nz - 1 if side else gz > 0
+            zpk[side] = jnp.where(inside, o + W * (pk[c, side] - (6.0 * o - s)), 0.0)
+        z = zfld[2 : bx + 2, 8 : 8 + by, :]
+        return z, jnp.stack([operate(zfld, zpk, i, 8, 8 + by) for i in range(2, bx + 2)])
 
     z0, w = cycle_and_image(0, r0)
     u, aw = cycle_and_image(1, w)
@@ -282,6 +323,9 @@
         lax.fori_loop(1, total, step, 0)
 
     share("start")
+    for c in (0, 1):
+        transfer(messages(c), "sent")
+        transfer(gathered(c), "sent")
     share("wait")
     tot = jnp.sum(sums[...], axis=0)
 
@@ -321,23 +365,28 @@
             in_specs=[vm] * 4,
             out_specs=(vm, vm),
             scratch_shapes=[
-                pltpu.VMEM((4, bx + 2, by + 16, bz), f32),
-                pltpu.VMEM((4, 2, bx, bz), f32),
-                pltpu.VMEM((4, 2, bx, bz), f32),
-                pltpu.VMEM((4, 2, by, bz), f32),
-                pltpu.VMEM((4, 2, by, bz), f32),
+                pltpu.VMEM((2, bx + 4, by + 16, bz), f32),
+                pltpu.VMEM((2, 2, 2, bx, bz), f32),
+                pltpu.VMEM((2, 2, 2, bx, bz), f32),
+                pltpu.VMEM((2, 2, 8, bz), f32),
+                pltpu.VMEM((2, 2, 5, 8, bz), f32),
                 pltpu.VMEM((hx, by, bz), f32),
                 pltpu.VMEM((hx + 2, by + 16, bz), f32),
                 pltpu.VMEM((2, hx, hy, bz), f32),
                 pltpu.VMEM((2, 3, (2 * kx + 1) * hx, (2 * ky + 1) * hy, bz), f32),
                 pltpu.VMEM((total, 1, bz), f32),
-                dma((4, 6)),
-                dma((4, 6)),
+                dma((2, 18)),
+                dma((2, 18)),
                 dma((2, near)),
                 dma((2, near)),
                 dma((total,)),
                 dma((total,)),
-                pltpu.VMEM((bx + 2, by + 16, bz), f32),
+                pltpu.VMEM((2, 4, bx, bz), f32),
+                pltpu.VMEM((2, 2, by + 16, bz), f32),
+                pltpu.VMEM((bx + 4, by + 16, bz), f32),
+                pltpu.VMEM((2, by + 16, bz), f32),
+                pltpu.VMEM((bx + 4, by + 16, bz), f32),
+                pltpu.VMEM((2, by + 16, bz), f32),
             ],
             compiler_params=pltpu.CompilerParams(collective_id=0, has_side_effects=True),
         )(density, x_faces, y_faces, z_faces)

time: 43.4 us -> 40 us (0.922)
  Pallas kernels: 40.4 us -> 37 us
    pallas_call x1, Pallas kernels: 40.4 us -> 37 us  [local(): pl.pallas_call(functools.partial(kernel, ns, bx, by, bz, kx, ky), out_sha...]
where the time goes in v2:
time: 40 us; the launch traced here: 39.7 us
  Pallas kernels  37 us (92%)
  local copies, waits for them, and re-layouts  2.14 us (5%)
  between operations  0.65 us (2%)
    pallas_call x1, Pallas kernels, local(): pl.pallas_call(functools.partial(kernel, ns, bx, by, bz, kx, ky), out_sha...  37 us
    unnamed x4, local copies, waits for them, and re-layouts  2.14 us

profile of v2, /device:TPU:0, one launch (start us, length us, event | category | flops | bytes accessed | tf_op | source)
XLA Modules:
  0.0 39.7 jit_solution(2663620993024507480)
XLA Ops:
  0.6 37.0 %shard_map.59 = (f32[8,16,128]{2,1,0:T(8,128)}, f32[8,16,128]{2,1,0:T(8,128)}) custom-call(f32[8,16,128]{2,1,0:T(8,128)} %den.1, f32[2,16,128]{2,1,0:T(8,128)} %xf.1, f32[2,8,128]{2,1,0:T(8,128)} %yf.1, f32[2,8,16]{2,1,0:T(8,128)} %zf.1), custom_call_target="tpu_custom_call" | custom-call | tf_op jit(solution)/shard_map/pallas_call | solution.py:362
  37.6 0.0 copy-start
  37.6 1.5 %copy.8 = f32[8,16,128]{2,1,0:T(8,128)} copy(f32[8,16,128]{2,1,0:T(8,128)} %get-tuple-element.4) | data formatting | bytes 131072
  39.1 0.0 copy-done
  39.1 0.6 %copy.9 = f32[8,16,128]{2,1,0:T(8,128)} copy(f32[8,16,128]{2,1,0:T(8,128)S(1)} %copy-done) | data formatting | bytes 131072
Async XLA Ops:
  37.6 1.5 %copy-start = (f32[8,16,128]{2,1,0:T(8,128)S(1)}, f32[8,16,128]{2,1,0:T(8,128)}, u32[]{:S(2)}) copy-start(f32[8,16,128]{2,1,0:T(8,128)} %get-tuple-element.5) | copy-start | bytes 196612

commit v3 on v2

--- a/solution.py
+++ b/solution.py
@@ -23,10 +23,10 @@
 
 def kernel(
     ns, bx, by, bz, kx, ky,
-    den, xf, yf, zf, sol, res,
-    fld, ysrc, yrec, zsrc, zrec, tmp, prol, dsrc, win, sums,
+    den_in, xf_in, yf_in, zf_in, sol, res,
+    fld, ysrc, yrec, zsrc, zrec, tmp, prol, dsrc, dside, win, wside, sums,
     fsend, frecv, dsend, drecv, ssend, srecv,
-    xyrec, pk, vfld, vpk, zfld, zpk,
+    xyrec, pk, vfld, vpk, zfld, zpk, den, xf, yf, zf, isem,
 ):
     nx, ny, nz = ns
     gx, gy, gz = (lax.axis_index(a) for a in ("gx", "gy", "gz"))
@@ -35,10 +35,18 @@
     total = nx * ny * nz
     f32 = jnp.float32
 
+    loads = [
+        pltpu.make_async_copy(a, b, isem.at[i])
+        for i, (a, b) in enumerate(((den_in, den), (xf_in, xf), (yf_in, yf), (zf_in, zf)))
+    ]
+    for load in loads:
+        load.start()
+
     fld[...] = jnp.zeros_like(fld)
     yrec[...] = jnp.zeros_like(yrec)
     zrec[...] = jnp.zeros_like(zrec)
     win[...] = jnp.zeros_like(win)
+    wside[...] = jnp.zeros_like(wside)
     xyrec[...] = jnp.zeros_like(xyrec)
     pk[...] = jnp.zeros_like(pk)
 
@@ -53,6 +61,9 @@
         return c
 
     lax.fori_loop(1, total, greet, 0)
+
+    for load in loads:
+        load.wait()
 
     lane = lane_of((by, bz))
     eye = lax.broadcasted_iota(jnp.int32, (by, by), 0) == lax.broadcasted_iota(jnp.int32, (by, by), 1)
@@ -71,8 +82,6 @@
             r = r + jnp.where((lane == at) & (gz == edge), col, 0.0)
         planes.append(r)
     r0 = jnp.stack(planes)
-
-    pl.semaphore_wait(barrier, total - 1)
 
     lane8 = lane_of((8, bz))
     lanef = lane_of((by + 16, bz))
@@ -142,6 +151,8 @@
                     out = jnp.where(lane8 // 2 == to // 2, moved, out)
             zsrc[c, side] = out
         items = messages(c)
+        if c == 0:
+            pl.semaphore_wait(barrier, total - 1)
         transfer(items, "start")
         transfer(items, "here")
         for p in range(bx):
@@ -184,8 +195,15 @@
         items = []
         for dx, dy, dz in offsets:
             i = ((dx + kx) * (2 * ky + 1) + dy + ky) * 3 + dz + 1
-            dst = win.at[c, 1 - dz, pl.ds((kx - dx) * hx, hx), pl.ds((ky - dy) * hy, hy)]
-            items.append(((dx, dy, dz), dsrc.at[c], dst, dsend.at[c, i], drecv.at[c, i]))
+            rows = pl.ds((ky - dy) * hy, hy)
+            if dz == 0:
+                n = hx // 2
+                src, dst = dsrc.at[c], win.at[c, pl.ds((kx - dx) * n, n), rows]
+            else:
+                n = hx // 4
+                side = (1 - dz) // 2
+                src, dst = dside.at[c, 1 - side], wside.at[c, side, pl.ds((kx - dx) * n, n), rows]
+            items.append(((dx, dy, dz), src, dst, dsend.at[c, i], drecv.at[c, i]))
         return items
 
     wx, wy = (2 * kx + 1) * hx, (2 * ky + 1) * hy
@@ -217,8 +235,15 @@
 
     def coarse(c):
         a0, a1 = ex - REACH, ex + hx + REACH
-        zi = lane_of((a1 - a0, wy, bz))
-        d = jnp.where(zi < q, win[c, 0, a0:a1], jnp.where(zi < q + hz, win[c, 1, a0:a1], win[c, 2, a0:a1]))
+        zi = lane_of((wy, bz))
+        d = []
+        for p in range(a0, a1):
+            t, l, h = win[c, p // 2], wside[c, 0, p // 4], wside[c, 1, p // 4]
+            t = roll(t, hz, 1) if p % 2 else t
+            l = roll(l, -q * (p % 4), 1) if p % 4 else l
+            h = roll(h, q + hz - q * (p % 4), 1) if p % 4 != 3 else h
+            d.append(jnp.where(zi < q, l, jnp.where(zi < q + hz, t, h)))
+        d = jnp.stack(d)
         v = W * d
         defect = d[1:-1] - (6.0 * v[1:-1] - beside(v, 1))
         n = defect.shape[0] // 2
@@ -243,7 +268,15 @@
     lj = lax.broadcasted_iota(jnp.int32, (bz, bz), 1)
     shrink = jnp.where(li // 2 == (lj - q + hz) % hz, 0.5, 0.0).astype(f32)
     grow = jnp.where(li == q + lj // 2, 1.0, 0.0).astype(f32)
-    dot = functools.partial(jnp.dot, precision=lax.Precision.HIGHEST, preferred_element_type=f32)
+
+    def dot(x, m):
+        out = None
+        for _ in range(3):
+            part = x.astype(jnp.bfloat16)
+            x = x - part.astype(f32)
+            y = jnp.dot(part, m.astype(jnp.bfloat16), preferred_element_type=f32)
+            out = y if out is None else out + y
+        return out
 
     def cycle_and_image(c, r):
         exchange(c, r)
@@ -255,8 +288,19 @@
             tmp[j] = d
         half = tmp[:, pl.ds(0, hy, stride=2), :] + tmp[:, pl.ds(1, hy, stride=2), :]
         d1 = dot(half.reshape(hx * hy, bz), shrink).reshape(hx, hy, bz)
-        dsrc[c] = d1
-        win[c, 1, ex : ex + hx, ey : ey + hy, :] = d1
+        li = lane_of((hy, bz))
+        for j in range(hx // 2):
+            t = jnp.where((li >= q) & (li < q + hz), d1[2 * j], d1[2 * j + 1])
+            dsrc[c, j] = t
+            win[c, ex // 2 + j, ey : ey + hy, :] = t
+        for j in range(hx // 4):
+            lo, hi = d1[4 * j], d1[4 * j]
+            lo = roll(lo, q, 1)
+            for m in range(1, 4):
+                lo = jnp.where(li // q == m, roll(d1[4 * j + m], q * (m + 1), 1), lo)
+                hi = jnp.where(li // q == m, roll(d1[4 * j + m], q * m, 1), hi)
+            dside[c, 0, j] = lo
+            dside[c, 1, j] = hi
         transfer(gathered(c), "start")
         transfer(gathered(c), "here")
         e1, p0 = coarse(c)
@@ -362,7 +406,7 @@
         return pl.pallas_call(
             functools.partial(kernel, ns, bx, by, bz, kx, ky),
             out_shape=(jax.ShapeDtypeStruct(density.shape, f32),) * 2,
-            in_specs=[vm] * 4,
+            in_specs=[pl.BlockSpec(memory_space=pl.ANY)] * 4,
             out_specs=(vm, vm),
             scratch_shapes=[
                 pltpu.VMEM((2, bx + 4, by + 16, bz), f32),
@@ -372,8 +416,10 @@
                 pltpu.VMEM((2, 2, 5, 8, bz), f32),
                 pltpu.VMEM((hx, by, bz), f32),
                 pltpu.VMEM((hx + 2, by + 16, bz), f32),
-                pltpu.VMEM((2, hx, hy, bz), f32),
-                pltpu.VMEM((2, 3, (2 * kx + 1) * hx, (2 * ky + 1) * hy, bz), f32),
+                pltpu.VMEM((2, hx // 2, hy, bz), f32),
+                pltpu.VMEM((2, 2, hx // 4, hy, bz), f32),
+                pltpu.VMEM((2, (2 * kx + 1) * hx // 2, (2 * ky + 1) * hy, bz), f32),
+                pltpu.VMEM((2, 2, (2 * kx + 1) * hx // 4, (2 * ky + 1) * hy, bz), f32),
                 pltpu.VMEM((total, 1, bz), f32),
                 dma((2, 18)),
                 dma((2, 18)),
@@ -387,6 +433,11 @@
                 pltpu.VMEM((2, by + 16, bz), f32),
                 pltpu.VMEM((bx + 4, by + 16, bz), f32),
                 pltpu.VMEM((2, by + 16, bz), f32),
+                pltpu.VMEM(density.shape, f32),
+                pltpu.VMEM(x_faces.shape, f32),
+                pltpu.VMEM(y_faces.shape, f32),
+                pltpu.VMEM(z_faces.shape, f32),
+                dma((4,)),
             ],
             compiler_params=pltpu.CompilerParams(collective_id=0, has_side_effects=True),
         )(density, x_faces, y_faces, z_faces)

time: 40 us -> 35.9 us (0.90)
  Pallas kernels: 37 us -> 33 us
    pallas_call x1, Pallas kernels: 37 us -> 33 us  [local(): pl.pallas_call(functools.partial(kernel, ns, bx, by, bz, kx, ky), out_sha...]
where the time goes in v3:
time: 35.9 us; the launch traced here: 35.8 us
  Pallas kernels  33 us (92%)
  local copies, waits for them, and re-layouts  2.14 us (6%)
  between operations  0.65 us (2%)
    pallas_call x1, Pallas kernels, local(): pl.pallas_call(functools.partial(kernel, ns, bx, by, bz, kx, ky), out_sha...  33 us
    unnamed x4, local copies, waits for them, and re-layouts  2.14 us

profile of v3, /device:TPU:0, one launch (start us, length us, event | category | flops | bytes accessed | tf_op | source)
XLA Modules:
  0.0 35.8 jit_solution(11148999964064963551)
XLA Ops:
  0.6 33.0 %shard_map.59 = (f32[8,16,128]{2,1,0:T(8,128)}, f32[8,16,128]{2,1,0:T(8,128)}) custom-call(f32[8,16,128]{2,1,0:T(8,128)} %den_in.1, f32[2,16,128]{2,1,0:T(8,128)} %xf_in.1, f32[2,8,128]{2,1,0:T(8,128)} %yf_in.1, f32[2,8,16]{2,1,0:T(8,128)} %zf_in.1), custom_call_target="tpu_custom_call" | custom-call | tf_op jit(solution)/shard_map/pallas_call | solution.py:406
  33.6 0.0 copy-start
  33.6 1.5 %copy.8 = f32[8,16,128]{2,1,0:T(8,128)} copy(f32[8,16,128]{2,1,0:T(8,128)} %get-tuple-element.4) | data formatting | bytes 131072
  35.1 0.0 copy-done
  35.1 0.6 %copy.9 = f32[8,16,128]{2,1,0:T(8,128)} copy(f32[8,16,128]{2,1,0:T(8,128)S(1)} %copy-done) | data formatting | bytes 131072
Async XLA Ops:
  33.6 1.5 %copy-start = (f32[8,16,128]{2,1,0:T(8,128)S(1)}, f32[8,16,128]{2,1,0:T(8,128)}, u32[]{:S(2)}) copy-start(f32[8,16,128]{2,1,0:T(8,128)} %get-tuple-element.5) | copy-start | bytes 196612
